TPU v7x, 32 devices: a whole 2x2x4 slice. The times are simulated.
32 devices in a mesh: lat: 8 (over z, y), lon: 4 (over x, core).
Axes of the slice: x: 2, y: 2, z: 4, core: 2. Of those that a mesh axis runs over, the one named last changes fastest.
Arguments:
- grid_latent: bfloat16 [16384, 512], P(('lat', 'lon')), may hold values from -6 to 6
- grid_feat: bfloat16 [4, 65536], P(None, ('lat', 'lon')), may hold values from -6 to 6
- grid_sender: int32 [65536], P(('lat', 'lon')), may hold values from 0 to 511
- grid_owner: int32 [65536, 1], P(('lat', 'lon')), may hold values from 0 to 7; in each aligned block of 2048 rows (0 to 2047, 2048 to 4095, ...) at most 512 rows name the same one
- grid_node: int32 [65536], P(('lat', 'lon')), may hold values from 0 to 511
- mesh_latent: bfloat16 [4096, 512], P('lat', 'lon'), may hold values from -6 to 6
- mesh_edge: bfloat16 [32768, 512], P(('lat', 'lon')), may hold values from -6 to 6
- halo_send: int32 [64, 64], P('lat'), may hold values from 0 to 511
- mesh_sender: int32 [32768], P(('lat', 'lon')), may hold values from 0 to 1023
- mesh_receiver: int32 [32768], P(('lat', 'lon')), may hold values from 0 to 511
- enc_edge_in: bfloat16 [512, 512], P(None, 'lon'), may hold values from -0.25 to 0.25
- enc_feat_proj: bfloat16 [4, 512], replicated, may hold values from -3 to 3
- enc_edge_out: bfloat16 [512, 512], P(None, 'lon'), may hold values from -0.25 to 0.25
- enc_edge_bias: float32 [2, 512], replicated, may hold values from -1.5 to 1.5
- enc_edge_gain: float32 [512], replicated, may hold values from 0.25 to 1.75
- enc_node_in: bfloat16 [1024, 512], P(None, 'lon'), may hold values from -0.1875 to 0.1875
- enc_node_out: bfloat16 [512, 512], P('lon'), may hold values from -0.25 to 0.25
- enc_node_bias: float32 [2, 512], replicated, may hold values from -1.5 to 1.5
- enc_node_gain: float32 [512], replicated, may hold values from 0.25 to 1.75
- proc_edge_in: bfloat16 [1536, 512], P(None, 'lon'), may hold values from -0.15625 to 0.15625
- proc_edge_out: bfloat16 [512, 512], P(None, 'lon'), may hold values from -0.25 to 0.25
- proc_edge_bias: float32 [2, 512], replicated, may hold values from -1.5 to 1.5
- proc_edge_gain: float32 [512], replicated, may hold values from 0.25 to 1.75
- proc_node_in: bfloat16 [1024, 512], P(None, 'lon'), may hold values from -0.1875 to 0.1875
- proc_node_out: bfloat16 [512, 512], P('lon'), may hold values from -0.25 to 0.25
- proc_node_bias: float32 [2, 512], replicated, may hold values from -1.5 to 1.5
- proc_node_gain: float32 [512], replicated, may hold values from 0.25 to 1.75
Outputs:
- mesh_update: bfloat16 [4096, 512], P('lat', 'lon')
- edge_update: bfloat16 [32768, 512], P(('lat', 'lon'))
Inputs may be any that keep to these rules, and one draw needn't show every extreme that they name: `grid_sender`: a row among the 512 grid rows of the device that holds the edge. `grid_owner`: among the 2048 edges of one device, at most 512 name the same partition, a bound that some block reaches. `halo_send`: nodes of the listing partition.
All inputs are finite; a program needn't handle non-finite values.
Results may differ from a plain program's by a relative error of at most 0.017.
Values may be sent and summed in bfloat16 or wider, within the bound.
No kernel may reach another device: no remote copies, remote signals or barrier semaphores. Data moves between devices by JAX's collectives and lax.ppermute only.
A program may use at most 128 MiB of HBM per device.

v0:
```python
import jax
import jax.numpy as jnp
from jax import lax
from jax.sharding import PartitionSpec as P


def layer_norm(values, norm_gain, offsets):
    average = jnp.mean(values, axis=-1, keepdims=True)
    centred = values - average
    spread = jnp.mean(centred * centred, axis=-1, keepdims=True)
    return centred * lax.rsqrt(spread + 1e-05) * norm_gain + offsets


def encoder_edges(source_rows, feat_term, weight_in, weight_out):
    piece_in = lax.all_gather(weight_in, "lon", axis=1, tiled=True)
    piece_out = lax.all_gather(weight_out, "lon", axis=1, tiled=True)
    pre_act = jnp.dot(source_rows, piece_in, preferred_element_type=jnp.float32)
    pre_act = pre_act + feat_term
    hidden = jax.nn.silu(pre_act).astype(jnp.bfloat16)
    return lax.dot_general(
        hidden, piece_out, (((1,), (1,)), ((), ())), preferred_element_type=jnp.float32
    )


def node_network(base, aggregate, weight_in, weight_out, biases, norm_gain):
    inputs = jnp.concatenate([base, aggregate], 1)
    columns = weight_in.shape[1]
    hidden_bias = lax.dynamic_slice_in_dim(biases[0], lax.axis_index("lon") * columns, columns)
    hidden = jax.nn.silu(
        jnp.dot(inputs, weight_in, preferred_element_type=jnp.float32) + hidden_bias
    ).astype(jnp.bfloat16)
    raw_out = lax.psum(
        jnp.dot(hidden, weight_out, preferred_element_type=jnp.float32).astype(jnp.bfloat16), "lon"
    ).astype(jnp.float32)
    return (base.astype(jnp.float32) + layer_norm(raw_out, norm_gain, biases[1])).astype(
        jnp.bfloat16
    )


def local(
    grid_latent,
    grid_feat,
    grid_sender,
    grid_owner,
    grid_node,
    mesh_latent,
    mesh_edge,
    halo_send,
    mesh_sender,
    mesh_receiver,
    enc_edge_in,
    enc_feat_proj,
    enc_edge_out,
    enc_edge_bias,
    enc_edge_gain,
    enc_node_in,
    enc_node_out,
    enc_node_bias,
    enc_node_gain,
    proc_edge_in,
    proc_edge_out,
    proc_edge_bias,
    proc_edge_gain,
    proc_node_in,
    proc_node_out,
    proc_node_bias,
    proc_node_gain,
):
    lat_count = lax.axis_size("lat")
    lon_index = lax.axis_index("lon")
    feature_width = grid_latent.shape[1]
    quarter = mesh_latent.shape[1]
    mesh_rows = mesh_latent.shape[0]
    edge_count = grid_sender.shape[0]
    capacity = max(2, 2 * edge_count // lat_count)
    slot_total = lat_count * capacity
    owners = grid_owner[:, 0]
    owner_hits = (owners[:, None] == jnp.arange(lat_count, dtype=jnp.int32)[None, :]).astype(
        jnp.int32
    )
    slot_rank = jnp.sum((jnp.cumsum(owner_hits, axis=0) - owner_hits) * owner_hits, axis=1)
    slot_index = owners * capacity + slot_rank
    node_slots = (
        jnp.full((slot_total,), -1, jnp.int32)
        .at[slot_index]
        .set(grid_node)
        .reshape(lat_count, capacity)
    )
    row_buffer = (
        jnp.zeros((slot_total, feature_width), jnp.bfloat16)
        .at[slot_index]
        .set(grid_latent[grid_sender])
    )
    feat_buffer = (
        jnp.zeros((slot_total, grid_feat.shape[0]), jnp.bfloat16).at[slot_index].set(grid_feat.T)
    )
    got_rows, got_feats, node_ids = (
        lax.all_to_all(
            row_buffer.reshape(lat_count, capacity, feature_width),
            "lat",
            split_axis=0,
            concat_axis=0,
            tiled=True,
        ),
        lax.all_to_all(
            feat_buffer.reshape(lat_count, capacity, grid_feat.shape[0]),
            "lat",
            split_axis=0,
            concat_axis=0,
            tiled=True,
        ),
        lax.all_to_all(node_slots, "lat", split_axis=0, concat_axis=0, tiled=True),
    )
    got_rows = got_rows.reshape(slot_total, feature_width)
    got_feats = got_feats.reshape(slot_total, grid_feat.shape[0])
    feat_term = (
        jnp.dot(got_feats, enc_feat_proj, preferred_element_type=jnp.float32) + enc_edge_bias[0]
    )
    raw_out = encoder_edges(got_rows, feat_term, enc_edge_in, enc_edge_out)
    arrived = layer_norm(raw_out, enc_edge_gain, enc_edge_bias[1])
    node_ids = node_ids.reshape(slot_total)
    segment_ids = jnp.where(node_ids < 0, mesh_rows, node_ids).astype(jnp.int32)
    partial_sum = jax.ops.segment_sum(arrived, segment_ids, num_segments=mesh_rows + 1)[:mesh_rows]
    gathered = lax.psum(partial_sum.astype(jnp.bfloat16), "lon")
    mesh_full = lax.all_gather(mesh_latent, "lon", axis=1, tiled=True)
    mesh_mid = node_network(
        mesh_full, gathered, enc_node_in, enc_node_out, enc_node_bias, enc_node_gain
    )
    outgoing = mesh_mid[halo_send]
    received = lax.all_to_all(outgoing, "lat", split_axis=0, concat_axis=0, tiled=True)
    table = jnp.concatenate([mesh_mid, received.reshape(-1, feature_width)], 0)
    sender_rows = table[mesh_sender]
    receiver_rows = mesh_mid[mesh_receiver]
    piece_in = lax.all_gather(proc_edge_in, "lon", axis=1, tiled=True)
    piece_out = lax.all_gather(proc_edge_out, "lon", axis=1, tiled=True)
    pre_act = jnp.dot(mesh_edge, piece_in[:feature_width], preferred_element_type=jnp.float32)
    pre_act = pre_act + jnp.dot(
        sender_rows, piece_in[feature_width : 2 * feature_width], preferred_element_type=jnp.float32
    )
    pre_act = pre_act + jnp.dot(
        receiver_rows, piece_in[2 * feature_width :], preferred_element_type=jnp.float32
    )
    pre_act = pre_act + proc_edge_bias[0]
    hidden = jax.nn.silu(pre_act).astype(jnp.bfloat16)
    edge_raw = lax.dot_general(
        hidden, piece_out, (((1,), (1,)), ((), ())), preferred_element_type=jnp.float32
    )
    edge_update = (
        mesh_edge.astype(jnp.float32) + layer_norm(edge_raw, proc_edge_gain, proc_edge_bias[1])
    ).astype(jnp.bfloat16)
    edge_onehot = (
        jnp.arange(mesh_rows, dtype=jnp.int32)[:, None] == mesh_receiver[None, :]
    ).astype(jnp.bfloat16)
    incoming = lax.psum(
        jnp.dot(edge_onehot, edge_update, preferred_element_type=jnp.float32).astype(jnp.bfloat16),
        "lon",
    )
    mesh_new = node_network(
        mesh_mid, incoming, proc_node_in, proc_node_out, proc_node_bias, proc_node_gain
    )
    mesh_update = lax.dynamic_slice_in_dim(mesh_new, lon_index * quarter, quarter, 1)
    return (mesh_update, edge_update)


def solution(mesh):
    placed = (
        P(("lat", "lon"), None),
        P(None, ("lat", "lon")),
        P(("lat", "lon")),
        P(("lat", "lon"), None),
        P(("lat", "lon")),
        P("lat", "lon"),
        P(("lat", "lon"), None),
        P("lat", None),
        P(("lat", "lon")),
        P(("lat", "lon")),
        P(None, "lon"),
        P(),
        P(None, "lon"),
        P(),
        P(),
        P(None, "lon"),
        P("lon", None),
        P(),
        P(),
        P(None, "lon"),
        P(None, "lon"),
        P(),
        P(),
        P(None, "lon"),
        P("lon", None),
        P(),
        P(),
    )
    return jax.shard_map(
        local,
        mesh=mesh,
        in_specs=placed,
        out_specs=(P("lat", "lon"), P(("lat", "lon"), None)),
        check_vma=False,
    )
```

profile of v0, /device:TPU:0, one launch (start us, length us, event | category | flops | bytes accessed | tf_op | source)
XLA Modules:
  0.0 417.4 jit_solution(599329200880381121)
XLA Ops:
  7.2 0.8 fusion.52
  7.9 2.3 reduce-window.6
  10.2 0.3 slice_reduce_fusion
  10.5 0.2 reduce-window.9
  10.7 0.1 add_bitcast_fusion
  10.8 0.7 fusion.51
  11.5 0.7 compare_select_fusion.1
  12.2 8.8 %scatter_custom_fusion = s32[4096]{0:T(1024)} fusion(s32[2048]{0:T(1024)S(1)} %bitcast.71, s32[2048]{0:T(1024)} %param.31, s32[]{:T(128)} %constant.19.clone.1), kind=kCustom, calls=%fused_computation.87 | custom fusion | bytes 16896 | tf_op jit(solution)/shard_map/scatter | solution.py:86
  21.0 7.3 %all-to-all-start = ((s32[8,1,512]{2,1,0:T(1,128)}), s32[8,1,512]{2,1,0:T(1,128)S(1)}, u32[]{:S(2)}, u32[]{:S(2)}) async-start(s32[8,1,512]{2,1,0:T(1,128)} %bitcast.5), calls=%async_computation | async-start | bytes 32768 | tf_op jit(solution)/shard_map/all_to_all | solution.py:112
  28.3 0.7 fusion.53
  29.0 21.3 %scatter_custom_fusion.1 = bf16[4096,512]{1,0:T(8,128)(2,1)} fusion(s32[2048]{0:T(1024)S(1)} %bitcast.72, bf16[512,512]{1,0:T(8,128)(2,1)S(1)} %copy-done, s32[2048]{0:T(1024)S(1)} %fusion.53, bf16[]{:T(256)} %constant.23.clone.1), kind=kCustom, calls=%fused_computation.11 | custom fusion | bytes 4194306 | tf_op jit(solution)/shard_map/scatter | solution.py:92
  50.3 6.1 %all-to-all-start.1 = ((bf16[8,512,512]{2,1,0:T(8,128)(2,1)}), bf16[8,512,512]{2,1,0:T(8,128)(2,1)}, u32[]{:S(2)}, u32[]{:S(2)}) async-start(bf16[8,512,512]{2,1,0:T(8,128)(2,1)} %bitcast.57), calls=%async_computation.1 | async-start | bytes 8388608 | tf_op jit(solution)/shard_map/all_to_all | solution.py:98
  56.5 0.3 copy.41
  56.8 6.1 %scatter_custom_fusion.2 = bf16[4096,4]{1,0:T(8,128)(2,1)S(1)} fusion(s32[2048]{0:T(1024)S(1)} %bitcast.73, bf16[2048,4]{1,0:T(8,128)(2,1)S(1)} %copy.41, bf16[]{:T(256)} %constant.23.clone.1), kind=kCustom, calls=%fused_computation.56 | custom fusion | bytes 32770 | tf_op jit(solution)/shard_map/scatter | solution.py:95
  62.9 1.0 copy.42
  63.9 7.2 %all_gather.16 = bf16[512,512]{1,0:T(8,128)(2,1)S(1)} all-gather(bf16[512,128]{1,0:T(8,128)(2,1)S(1)} %copy-done.8), channel_id=1, replica_groups=mesh['lat'=8,'lon'=4] {'lon'}, dimensions={1}, use_global_device_ids=true | all-gather | bytes 655360 | tf_op jit(solution)/shard_map/all_gather | solution.py:15
  71.1 7.3 %all_gather.17 = bf16[512,512]{1,0:T(8,128)(2,1)S(1)} all-gather(bf16[512,128]{1,0:T(8,128)(2,1)S(1)} %copy-done.9), channel_id=1, replica_groups=mesh['lat'=8,'lon'=4] {'lon'}, dimensions={1}, use_global_device_ids=true | all-gather | bytes 655360 | tf_op jit(solution)/shard_map/all_gather | solution.py:16
  78.4 70.7 %all-to-all-done.1 = bf16[8,512,512]{2,1,0:T(8,128)(2,1)} async-done(((bf16[8,512,512]{2,1,0:T(8,128)(2,1)}), bf16[8,512,512]{2,1,0:T(8,128)(2,1)}, u32[]{:S(2)}, u32[]{:S(2)}) %all-to-all-start.1) | async-done | bytes 4194336 | tf_op jit(solution)/shard_map/all_to_all | solution.py:98
  149.2 3.6 all-to-all-start.2
  152.8 0.2 all-reduce.5.cloned.1.call-start
  153.0 7.7 %fusion.76 = f32[4096,512]{1,0:T(8,128)} fusion(bf16[4096,512]{1,0:T(8,128)(2,1)} %bitcast.9, bf16[512,512]{1,0:T(8,128)(2,1)S(1)} %all_gather.16), kind=kOutput, calls=%fused_computation.114 | convolution fusion | flops 2147483648 | bytes 13107200 | tf_op jit(solution)/shard_map/dot_general | solution.py:17
  160.8 8.9 %fusion.72 = (f32[4096]{0:T(1024)S(1)}, f32[4096,512]{0,1:T(8,128)}) fusion(bf16[512,512]{1,0:T(8,128)(2,1)S(1)} %all_gather.17, f32[4096,512]{1,0:T(8,128)} %fusion.76, bf16[4096,4]{0,1:T(4,128)(2,1)S(1)} %bitcast.64, bf16[4,512]{1,0:T(4,128)(2,1)S(1)} %copy-done.27, f32[512]{0:T(512)S(1)} %bitcast.74), kind=kOutput, calls=%fused_computation.112 | convolution fusion | flops 2181033984 | bytes 17356800 | tf_op jit(solution)/shard_map/dot_general | solution.py:20
  169.7 4.5 %multiply_reduce_fusion = f32[4096]{0:T(1024)S(1)} fusion(f32[4096,512]{0,1:T(8,128)} %get-tuple-element.21, f32[4096]{0:T(1024)S(1)} %broadcast_multiply_fusion), kind=kLoop, calls=%fused_computation.9 | loop fusion | flops 6287360 | bytes 8421376 | tf_op jit(solution)/shard_map/reduce_sum | solution.py:10
  174.3 1.2 copy-done.2
  175.5 5.1 %multiply_add_fusion = f32[4096,512]{0,1:T(8,128)} fusion(f32[4096,512]{0,1:T(8,128)S(1)} %copy-done.2, f32[512]{0:T(512)S(1)} %bitcast.70, f32[512]{0:T(512)S(1)} %copy-done.21, f32[4096]{0:T(1024)S(1)} %add_rsqrt_fusion, f32[4096]{0:T(1024)S(1)} %broadcast_multiply_fusion), kind=kLoop, calls=%fused_computation.8 | loop fusion | flops 8388608 | bytes 16814080 | tf_op jit(solution)/shard_map/add | solution.py:11
  180.6 9.0 %copy.43 = f32[4096,512]{1,0:T(8,128)} copy(f32[4096,512]{0,1:T(8,128)} %multiply_add_fusion) | data formatting | bytes 16777216 | tf_op jit(solution)/shard_map/add | solution.py:11
  189.6 25.5 %scatter_custom_fusion.3 = f32[513,512]{1,0:T(8,128)S(1)} fusion(s32[4096]{0:T(1024)S(1)} %bitcast.67, f32[4096,512]{1,0:T(8,128)} %copy.43, f32[]{:T(128)} %constant.18.clone.1), kind=kCustom, calls=%fused_computation.49 | custom fusion | flops 2097152 | bytes 1051136 | tf_op jit(solution)/shard_map/scatter-add | solution.py:123
  215.1 0.9 slice.81
  216.0 0.0 all-reduce.7.cloned.1.call-start
  216.1 7.2 %all_gather.15 = bf16[512,512]{1,0:T(8,128)(2,1)S(1)} all-gather(bf16[512,128]{1,0:T(8,128)(2,1)S(1)} %copy-done.10), channel_id=1, replica_groups=mesh['lat'=8,'lon'=4] {'lon'}, dimensions={1}, use_global_device_ids=true | all-gather | bytes 655360 | tf_op jit(solution)/shard_map/all_gather | solution.py:125
  223.3 30.2 %all-reduce.5.cloned.1.call-done = bf16[512,512]{1,0:T(8,128)(2,1)} async-done(((bf16[512,512]{1,0:T(8,128)(2,1)}), bf16[512,512]{1,0:T(8,128)(2,1)}) %all-reduce.5.cloned.1.call-update) | async-done | bytes 524304 | tf_op jit(solution)/shard_map/psum | solution.py:124
  253.5 2.4 convolution_convert_fusion.1
  255.9 0.3 all-gather.2.cloned.1.call-start
  256.2 0.5 all-gather.2.cloned.1.call-update
  256.7 0.1 reshape.137
  256.8 1.3 copy.44
  258.1 31.5 %all-reduce.7.cloned.1.call-done = bf16[512,512]{1,0:T(8,128)(2,1)} async-done(((bf16[512,512]{1,0:T(8,128)(2,1)}), bf16[512,512]{1,0:T(8,128)(2,1)}) %all-reduce.7.cloned.1.call-update) | async-done | bytes 524304 | tf_op jit(solution)/shard_map/psum | solution.py:32
  289.6 1.2 convert_reduce_fusion.1
  290.8 1.3 fusion.9
  292.1 1.4 fusion.13
  293.6 2.6 gather_fusion
  296.2 5.5 %all-to-all-start.3 = ((bf16[8,64,512]{2,1,0:T(8,128)(2,1)}), bf16[8,64,512]{2,1,0:T(8,128)(2,1)S(1)}, u32[]{:S(2)}, u32[]{:S(2)}) async-start(bf16[8,64,512]{2,1,0:T(8,128)(2,1)} %bitcast.17), calls=%async_computation.3 | async-start | bytes 1048576 | tf_op jit(solution)/shard_map/all_to_all | solution.py:130
  301.8 10.7 %all_gather.19 = bf16[512,512]{1,0:T(8,128)(2,1)} all-gather(bf16[512,128]{1,0:T(8,128)(2,1)S(1)} %copy-done.11), channel_id=1, replica_groups=mesh['lat'=8,'lon'=4] {'lon'}, dimensions={1}, use_global_device_ids=true | all-gather | bytes 655360 | tf_op jit(solution)/shard_map/all_gather | solution.py:135
  312.5 1.4 all-gather.2.cloned.1.call-done
  313.9 3.1 fusion.29
  317.0 5.1 %gather_fusion.2 = bf16[1024,512]{1,0:T(8,128)(2,1)} fusion(bf16[512,512]{1,0:T(8,128)(2,1)S(1)} %fusion.13, s32[1024]{0:T(1024)S(1)} %fusion.57), kind=kCustom, calls=%fused_computation.3 | custom fusion | bytes 2101248 | tf_op jit(solution)/shard_map/gather | solution.py:133
  322.1 0.1 pad_maximum_fusion
  322.2 4.0 gather_fusion.1
  326.2 3.1 fusion.27
  329.3 4.3 %fusion.73 = (f32[1024]{0:T(1024)S(1)}, f32[1024,512]{0,1:T(8,128)S(1)}) fusion(bf16[512,512]{1,0:T(8,128)(2,1)S(1)} %copy-done.7, f32[1024,512]{1,0:T(8,128)} %fusion.29, f32[1024,512]{1,0:T(8,128)} %fusion.27, bf16[1024,512]{1,0:T(8,128)(2,1)} %gather_fusion.2, f32[512]{0:T(512)S(1)} %bitcast.75, bf16[1536,512]{1,0:T(8,128)(2,1)} %all-gather.2.cloned.1.call-done), kind=kOutput, calls=%fused_computation.113 | convolution fusion | flops 1078459392 | bytes 8394752 | tf_op jit(solution)/shard_map/dot_general | solution.py:145
  333.6 0.3 multiply_reduce_fusion.1
  333.9 0.9 copy-done.4
  334.8 0.5 add_convert_fusion
  335.3 1.0 copy-done.5
  336.3 1.5 fusion.6
  337.9 33.4 %all-reduce.9.cloned.1.call-done = bf16[512,512]{1,0:T(8,128)(2,1)} async-done(((bf16[512,512]{1,0:T(8,128)(2,1)}), bf16[512,512]{1,0:T(8,128)(2,1)}) %all-reduce.9.cloned.1.call-update) | async-done | bytes 524304 | tf_op jit(solution)/shard_map/psum | solution.py:154
  371.4 2.4 convolution_convert_fusion
  373.8 0.1 dynamic-slice.3
  373.9 0.8 dynamic-slice.2
  374.7 1.3 copy.45
  376.0 31.5 %all-reduce.11.cloned.1.call-done = bf16[512,512]{1,0:T(8,128)(2,1)} async-done(((bf16[512,512]{1,0:T(8,128)(2,1)}), bf16[512,512]{1,0:T(8,128)(2,1)}) %all-reduce.11.cloned.1.call-update) | async-done | bytes 524304 | tf_op jit(solution)/shard_map/psum | solution.py:32
  407.5 1.2 convert_reduce_fusion
  408.7 1.3 multiply_reduce_fusion.2
  410.1 0.8 fusion.36
  (81 shorter events, 0.4 us)
Async XLA Ops:
  7.2 21.9 %copy-start = (bf16[512,512]{1,0:T(8,128)(2,1)S(1)}, bf16[512,512]{1,0:T(8,128)(2,1)}, u32[]{:S(2)}) copy-start(bf16[512,512]{1,0:T(8,128)(2,1)} %param.27) | copy-start | bytes 1572868
  21.0 29.3 %all-to-all-start = ((s32[8,1,512]{2,1,0:T(1,128)}), s32[8,1,512]{2,1,0:T(1,128)S(1)}, u32[]{:S(2)}, u32[]{:S(2)}) async-start(s32[8,1,512]{2,1,0:T(1,128)} %bitcast.5), calls=%async_computation | async-start | bytes 32768 | tf_op jit(solution)/shard_map/all_to_all | solution.py:112
  50.3 6.2 %copy-start.12 = (bf16[4,2048]{1,0:T(4,128)(2,1)S(1)}, bf16[4,2048]{1,0:T(4,128)(2,1)}, u32[]{:S(2)}) copy-start(bf16[4,2048]{1,0:T(4,128)(2,1)} %param.28) | copy-start | bytes 49156
  50.3 98.9 %all-to-all-start.1 = ((bf16[8,512,512]{2,1,0:T(8,128)(2,1)}), bf16[8,512,512]{2,1,0:T(8,128)(2,1)}, u32[]{:S(2)}, u32[]{:S(2)}) async-start(bf16[8,512,512]{2,1,0:T(8,128)(2,1)} %bitcast.57), calls=%async_computation.1 | async-start | bytes 8388608 | tf_op jit(solution)/shard_map/all_to_all | solution.py:98
  56.4 7.5 %copy-start.8 = (bf16[512,128]{1,0:T(8,128)(2,1)S(1)}, bf16[512,128]{1,0:T(8,128)(2,1)}, u32[]{:S(2)}) copy-start(bf16[512,128]{1,0:T(8,128)(2,1)} %param.37) | copy-start | bytes 393220
  56.4 14.7 %copy-start.9 = (bf16[512,128]{1,0:T(8,128)(2,1)S(1)}, bf16[512,128]{1,0:T(8,128)(2,1)}, u32[]{:S(2)}) copy-start(bf16[512,128]{1,0:T(8,128)(2,1)} %param.39) | copy-start | bytes 393220
  56.5 21.9 %copy-start.13 = (f32[2,512]{1,0:T(2,128)S(1)}, f32[2,512]{1,0:T(2,128)}, u32[]{:S(2)}) copy-start(f32[2,512]{1,0:T(2,128)} %param.40) | copy-start | bytes 12292
  56.5 21.9 %copy-start.14 = (f32[2,512]{1,0:T(2,128)S(1)}, f32[2,512]{1,0:T(2,128)}, u32[]{:S(2)}) copy-start(f32[2,512]{1,0:T(2,128)} %param.44) | copy-start | bytes 12292
  149.2 11.6 %all-to-all-start.2 = ((bf16[8,512,4]{1,2,0:T(4,128)(2,1)}), bf16[8,512,4]{1,2,0:T(4,128)(2,1)S(1)}, u32[]{:S(2)}, u32[]{:S(2)}) async-start(bf16[8,512,4]{1,2,0:T(4,128)(2,1)} %copy.42), calls=%async_computation.2 | async-start | bytes 65536 | tf_op jit(solution)/shard_map/all_to_all | solution.py:105
  152.8 100.7 %all-reduce.5.cloned.1.call-start = ((), (), s32[]{:S(2)}) async-start(), calls=%async_computation.4 | async-start | bytes 1048576 | tf_op jit(solution)/shard_map/psum | solution.py:124
  153.0 7.8 %copy-start.27 = (bf16[4,512]{1,0:T(4,128)(2,1)S(1)}, bf16[4,512]{1,0:T(4,128)(2,1)}, u32[]{:S(2)}) copy-start(bf16[4,512]{1,0:T(4,128)(2,1)} %param.38) | copy-start | bytes 12292
  169.7 5.8 %copy-start.2 = (f32[4096,512]{0,1:T(8,128)S(1)}, f32[4096,512]{0,1:T(8,128)}, u32[]{:S(2)}) copy-start(f32[4096,512]{0,1:T(8,128)} %get-tuple-element.21) | copy-start | bytes 25165828
  169.7 5.8 %copy-start.21 = (f32[512]{0:T(512)S(1)}, f32[512]{0:T(512)}, u32[]{:S(2)}) copy-start(f32[512]{0:T(512)} %param.41) | copy-start | bytes 6148
  189.6 26.5 %copy-start.10 = (bf16[512,128]{1,0:T(8,128)(2,1)S(1)}, bf16[512,128]{1,0:T(8,128)(2,1)}, u32[]{:S(2)}) copy-start(bf16[512,128]{1,0:T(8,128)(2,1)} %param.32) | copy-start | bytes 393220
  189.6 63.9 %copy-start.23 = (bf16[1024,128]{1,0:T(8,128)(2,1)S(1)}, bf16[1024,128]{1,0:T(8,128)(2,1)}, u32[]{:S(2)}) copy-start(bf16[1024,128]{1,0:T(8,128)(2,1)} %param.42) | copy-start | bytes 786436
  189.6 63.9 %copy-start.25 = (bf16[128,512]{1,0:T(8,128)(2,1)S(1)}, bf16[128,512]{1,0:T(8,128)(2,1)}, u32[]{:S(2)}) copy-start(bf16[128,512]{1,0:T(8,128)(2,1)} %param.43) | copy-start | bytes 393220
  216.0 73.6 %all-reduce.7.cloned.1.call-start = ((), (), s32[]{:S(2)}) async-start(), calls=%async_computation.5 | async-start | bytes 1048576 | tf_op jit(solution)/shard_map/psum | solution.py:32
  223.3 33.4 %copy-start.15 = (s32[8,64]{1,0:T(8,128)S(1)}, s32[8,64]{1,0:T(8,128)}, u32[]{:S(2)}) copy-start(s32[8,64]{1,0:T(8,128)} %param.34) | copy-start | bytes 6148
  223.3 33.5 %copy-start.3 = (bf16[1024,512]{1,0:T(8,128)(2,1)S(1)}, bf16[1024,512]{1,0:T(8,128)(2,1)}, u32[]{:S(2)}) copy-start(bf16[1024,512]{1,0:T(8,128)(2,1)} %param.33) | copy-start | bytes 3145732
  255.9 2.2 copy-start.16
  255.9 36.2 %copy-start.22 = (f32[512]{0:T(512)S(1)}, f32[512]{0:T(512)}, u32[]{:S(2)}) copy-start(f32[512]{0:T(512)} %param.45) | copy-start | bytes 6148
  255.9 58.0 %all-gather.2.cloned.1.call-start = ((), (), s32[]{:S(2)}) async-start(), calls=%async_computation.6 | async-start | bytes 1966080 | tf_op jit(solution)/shard_map/all_gather | solution.py:134
  293.5 8.2 %copy-start.11 = (bf16[512,128]{1,0:T(8,128)(2,1)S(1)}, bf16[512,128]{1,0:T(8,128)(2,1)}, u32[]{:S(2)}) copy-start(bf16[512,128]{1,0:T(8,128)(2,1)} %param.47) | copy-start | bytes 393220
  293.5 19.0 %copy-start.18 = (s32[1024]{0:T(1024)S(1)}, s32[1024]{0:T(1024)}, u32[]{:S(2)}) copy-start(s32[1024]{0:T(1024)} %param.36) | copy-start | bytes 12292
  293.5 19.0 %copy-start.17 = (f32[2,512]{1,0:T(2,128)S(1)}, f32[2,512]{1,0:T(2,128)}, u32[]{:S(2)}) copy-start(f32[2,512]{1,0:T(2,128)} %param.48) | copy-start | bytes 12292
  296.2 25.9 %all-to-all-start.3 = ((bf16[8,64,512]{2,1,0:T(8,128)(2,1)}), bf16[8,64,512]{2,1,0:T(8,128)(2,1)S(1)}, u32[]{:S(2)}, u32[]{:S(2)}) async-start(bf16[8,64,512]{2,1,0:T(8,128)(2,1)} %bitcast.17), calls=%async_computation.3 | async-start | bytes 1048576 | tf_op jit(solution)/shard_map/all_to_all | solution.py:130
  301.7 69.7 %all-reduce.9.cloned.1.call-start = ((), (), s32[]{:S(2)}) async-start(), calls=%async_computation.7 | async-start | bytes 1048576 | tf_op jit(solution)/shard_map/psum | solution.py:154
  326.1 3.1 copy-start.7
  333.5 1.2 copy-start.4
  333.6 1.2 copy-start.20
  335.3 1.0 copy-start.5
  336.3 1.6 copy-start.19
  336.3 35.1 %copy-start.24 = (bf16[1024,128]{1,0:T(8,128)(2,1)S(1)}, bf16[1024,128]{1,0:T(8,128)(2,1)}, u32[]{:S(2)}) copy-start(bf16[1024,128]{1,0:T(8,128)(2,1)} %param.50) | copy-start | bytes 786436
  336.3 35.1 %copy-start.26 = (bf16[128,512]{1,0:T(8,128)(2,1)S(1)}, bf16[128,512]{1,0:T(8,128)(2,1)}, u32[]{:S(2)}) copy-start(bf16[128,512]{1,0:T(8,128)(2,1)} %param.51) | copy-start | bytes 393220
  337.8 69.7 %all-reduce.11.cloned.1.call-start = ((), (), s32[]{:S(2)}) async-start(), calls=%async_computation.8 | async-start | bytes 1048576 | tf_op jit(solution)/shard_map/psum | solution.py:32
  337.9 36.8 %copy-start.6 = (bf16[1024,512]{0,1:T(8,128)(2,1)S(1)}, bf16[1024,512]{0,1:T(8,128)(2,1)}, u32[]{:S(2)}) copy-start(bf16[1024,512]{0,1:T(8,128)(2,1)} %copy-done.5) | copy-start | bytes 3145732
  373.9 37.0 %copy-start.1 = (bf16[512,512]{1,0:T(8,128)(2,1)S(1)}, bf16[512,512]{1,0:T(8,128)(2,1)}, u32[]{:S(2)}) copy-start(bf16[512,512]{1,0:T(8,128)(2,1)} %param.27) | copy-start | bytes 1572868
Sparse Core Ops, SparseCore 0:
  216.1 37.3 all-reduce.4
  256.1 33.4 all-reduce.6
  291.2 22.7 all-gather.1
  338.0 33.3 all-reduce.8
  374.0 33.5 all-reduce.10
where the time goes:
time: 419 us; the launch traced here: 417 us
  waiting for transfers between devices  199 us (47%)
  local copies, waits for them, and re-layouts  66.1 us (16%)
  other arithmetic  48.8 us (12%)
  matrix products  33.5 us (8%)
  blocking collectives  32.4 us (8%)
  starting transfers between devices  23.2 us (6%)
  between operations  14.2 us (3%)
    all_to_all x1, waiting for transfers between devices, local(): lax.all_to_all(row_buffer.reshape(lat_count, capacity, feature_width), 'l...  70.7 us
    psum x2, waiting for transfers between devices, node_network(): lax.psum(jnp.dot(hidden, weight_out, preferred_element_type=jnp.float32)....  63 us
    psum x1, waiting for transfers between devices, local(): lax.psum(jnp.dot(edge_onehot, edge_update, preferred_element_type=jnp.flo...  33.4 us
    psum x1, waiting for transfers between devices, local(): gathered = lax.psum(partial_sum.astype(jnp.bfloat16), 'lon')  30.2 us
    scatter-add x1, other arithmetic, local(): jax.ops.segment_sum(arrived, segment_ids, num_segments=mesh_rows + 1)  25.5 us
    scatter x1, local copies, waits for them, and re-layouts, local(): row_buffer = jnp.zeros((slot_total, feature_width), jnp.bfloat16).at[slot...  21.3 us
    all_gather x1, blocking collectives, local(): piece_out = lax.all_gather(proc_edge_out, 'lon', axis=1, tiled=True)  10.7 us
    add x1, local copies, waits for them, and re-layouts, layer_norm(): return centred * lax.rsqrt(spread + 1e-05) * norm_gain + offsets  8.98 us
  transfers between devices with their start and end apart: 9, of which 6 were waited for; matrix products, arithmetic and copies ran while one was open for 13% of the time, Pallas kernels for 0%

commit v1 on v0

--- a/solution.py
+++ b/solution.py
@@ -29,8 +29,12 @@
     hidden = jax.nn.silu(
         jnp.dot(inputs, weight_in, preferred_element_type=jnp.float32) + hidden_bias
     ).astype(jnp.bfloat16)
-    raw_out = lax.psum(
-        jnp.dot(hidden, weight_out, preferred_element_type=jnp.float32).astype(jnp.bfloat16), "lon"
+    raw_out = jnp.sum(
+        lax.all_gather(
+            jnp.dot(hidden, weight_out, preferred_element_type=jnp.float32).astype(jnp.bfloat16),
+            "lon",
+        ),
+        axis=0,
     ).astype(jnp.float32)
     return (base.astype(jnp.float32) + layer_norm(raw_out, norm_gain, biases[1])).astype(
         jnp.bfloat16

time: 419 us -> 397 us (0.947)
  waiting for transfers between devices: 199 us -> 178 us
    psum x2 -> x0, waiting for transfers between devices: 63 us -> none  [node_network(): lax.psum(jnp.dot(hidden, weight_out, preferred_element_type=jnp.float32)....]
    all_gather x0 -> x2, waiting for transfers between devices: none -> 41.3 us  [node_network(): lax.all_gather(jnp.dot(hidden, weight_out, preferred_element_type=jnp.flo...]
    reduce_sum x0 -> x2, other arithmetic: none -> 4.41 us  [node_network(): jnp.sum(lax.all_gather(jnp.dot(hidden, weight_out, preferred_element_type...]
  transfers between devices with their start and end apart: 9 -> 9, of which waited for: 6 -> 6; matrix products, arithmetic and copies ran while one was open for 13% -> 14% of each run, Pallas kernels for 0% -> 0%
where the time goes in v1:
time: 397 us; the launch traced here: 396 us
  waiting for transfers between devices  178 us (45%)
  local copies, waits for them, and re-layouts  66.1 us (17%)
  other arithmetic  48 us (12%)
  matrix products  33.5 us (8%)
  blocking collectives  32.6 us (8%)
  starting transfers between devices  23.2 us (6%)
  between operations  14.2 us (4%)
    all_to_all x1, waiting for transfers between devices, local(): lax.all_to_all(row_buffer.reshape(lat_count, capacity, feature_width), 'l...  70.7 us
    all_gather x2, waiting for transfers between devices, node_network(): lax.all_gather(jnp.dot(hidden, weight_out, preferred_element_type=jnp.flo...  41.3 us
    psum x1, waiting for transfers between devices, local(): lax.psum(jnp.dot(edge_onehot, edge_update, preferred_element_type=jnp.flo...  33.5 us
    psum x1, waiting for transfers between devices, local(): gathered = lax.psum(partial_sum.astype(jnp.bfloat16), 'lon')  30.2 us
    scatter-add x1, other arithmetic, local(): jax.ops.segment_sum(arrived, segment_ids, num_segments=mesh_rows + 1)  25.5 us
    scatter x1, local copies, waits for them, and re-layouts, local(): row_buffer = jnp.zeros((slot_total, feature_width), jnp.bfloat16).at[slot...  21.3 us
    all_gather x1, blocking collectives, local(): piece_out = lax.all_gather(proc_edge_out, 'lon', axis=1, tiled=True)  10.9 us
    add x1, local copies, waits for them, and re-layouts, layer_norm(): return centred * lax.rsqrt(spread + 1e-05) * norm_gain + offsets  8.98 us
  transfers between devices with their start and end apart: 9, of which 6 were waited for; matrix products, arithmetic and copies ran while one was open for 14% of the time, Pallas kernels for 0%

profile of v1, /device:TPU:0, one launch (start us, length us, event | category | flops | bytes accessed | tf_op | source)
XLA Modules:
  0.0 395.8 jit_solution(5510590718619167925)
XLA Ops:
  7.2 0.8 fusion.52
  7.9 2.3 reduce-window.6
  10.2 0.3 slice_reduce_fusion
  10.5 0.2 reduce-window.9
  10.7 0.1 add_bitcast_fusion
  10.8 0.7 fusion.51
  11.5 0.7 compare_select_fusion.1
  12.2 8.8 %scatter_custom_fusion = s32[4096]{0:T(1024)} fusion(s32[2048]{0:T(1024)S(1)} %bitcast.75, s32[2048]{0:T(1024)} %param.31, s32[]{:T(128)} %constant.21.clone.1), kind=kCustom, calls=%fused_computation.87 | custom fusion | bytes 16896 | tf_op jit(solution)/shard_map/scatter | solution.py:90
  21.0 7.3 %all-to-all-start = ((s32[8,1,512]{2,1,0:T(1,128)}), s32[8,1,512]{2,1,0:T(1,128)S(1)}, u32[]{:S(2)}, u32[]{:S(2)}) async-start(s32[8,1,512]{2,1,0:T(1,128)} %bitcast.5), calls=%async_computation | async-start | bytes 32768 | tf_op jit(solution)/shard_map/all_to_all | solution.py:116
  28.3 0.7 fusion.53
  29.0 21.3 %scatter_custom_fusion.1 = bf16[4096,512]{1,0:T(8,128)(2,1)} fusion(s32[2048]{0:T(1024)S(1)} %bitcast.76, bf16[512,512]{1,0:T(8,128)(2,1)S(1)} %copy-done, s32[2048]{0:T(1024)S(1)} %fusion.53, bf16[]{:T(256)} %constant.25.clone.1), kind=kCustom, calls=%fused_computation.11 | custom fusion | bytes 4194306 | tf_op jit(solution)/shard_map/scatter | solution.py:96
  50.3 6.1 %all-to-all-start.1 = ((bf16[8,512,512]{2,1,0:T(8,128)(2,1)}), bf16[8,512,512]{2,1,0:T(8,128)(2,1)}, u32[]{:S(2)}, u32[]{:S(2)}) async-start(bf16[8,512,512]{2,1,0:T(8,128)(2,1)} %bitcast.59), calls=%async_computation.1 | async-start | bytes 8388608 | tf_op jit(solution)/shard_map/all_to_all | solution.py:102
  56.5 0.3 copy.41
  56.8 6.1 %scatter_custom_fusion.2 = bf16[4096,4]{1,0:T(8,128)(2,1)S(1)} fusion(s32[2048]{0:T(1024)S(1)} %bitcast.77, bf16[2048,4]{1,0:T(8,128)(2,1)S(1)} %copy.41, bf16[]{:T(256)} %constant.25.clone.1), kind=kCustom, calls=%fused_computation.56 | custom fusion | bytes 32770 | tf_op jit(solution)/shard_map/scatter | solution.py:99
  62.9 1.0 copy.42
  63.9 7.2 %all_gather.28 = bf16[512,512]{1,0:T(8,128)(2,1)S(1)} all-gather(bf16[512,128]{1,0:T(8,128)(2,1)S(1)} %copy-done.8), channel_id=1, replica_groups=mesh['lat'=8,'lon'=4] {'lon'}, dimensions={1}, use_global_device_ids=true | all-gather | bytes 655360 | tf_op jit(solution)/shard_map/all_gather | solution.py:15
  71.1 7.3 %all_gather.29 = bf16[512,512]{1,0:T(8,128)(2,1)S(1)} all-gather(bf16[512,128]{1,0:T(8,128)(2,1)S(1)} %copy-done.9), channel_id=1, replica_groups=mesh['lat'=8,'lon'=4] {'lon'}, dimensions={1}, use_global_device_ids=true | all-gather | bytes 655360 | tf_op jit(solution)/shard_map/all_gather | solution.py:16
  78.4 70.7 %all-to-all-done.1 = bf16[8,512,512]{2,1,0:T(8,128)(2,1)} async-done(((bf16[8,512,512]{2,1,0:T(8,128)(2,1)}), bf16[8,512,512]{2,1,0:T(8,128)(2,1)}, u32[]{:S(2)}, u32[]{:S(2)}) %all-to-all-start.1) | async-done | bytes 4194336 | tf_op jit(solution)/shard_map/all_to_all | solution.py:102
  149.2 3.6 all-to-all-start.2
  152.8 0.2 all-reduce.3.cloned.1.call-start
  153.0 7.7 %fusion.76 = f32[4096,512]{1,0:T(8,128)} fusion(bf16[4096,512]{1,0:T(8,128)(2,1)} %bitcast.9, bf16[512,512]{1,0:T(8,128)(2,1)S(1)} %all_gather.28), kind=kOutput, calls=%fused_computation.114 | convolution fusion | flops 2147483648 | bytes 13107200 | tf_op jit(solution)/shard_map/dot_general | solution.py:17
  160.8 8.9 %fusion.72 = (f32[4096]{0:T(1024)S(1)}, f32[4096,512]{0,1:T(8,128)}) fusion(bf16[512,512]{1,0:T(8,128)(2,1)S(1)} %all_gather.29, f32[4096,512]{1,0:T(8,128)} %fusion.76, bf16[4096,4]{0,1:T(4,128)(2,1)S(1)} %bitcast.68, bf16[4,512]{1,0:T(4,128)(2,1)S(1)} %copy-done.27, f32[512]{0:T(512)S(1)} %bitcast.78), kind=kOutput, calls=%fused_computation.112 | convolution fusion | flops 2181033984 | bytes 17356800 | tf_op jit(solution)/shard_map/dot_general | solution.py:20
  169.7 4.5 %multiply_reduce_fusion = f32[4096]{0:T(1024)S(1)} fusion(f32[4096,512]{0,1:T(8,128)} %get-tuple-element.21, f32[4096]{0:T(1024)S(1)} %broadcast_multiply_fusion), kind=kLoop, calls=%fused_computation.9 | loop fusion | flops 6287360 | bytes 8421376 | tf_op jit(solution)/shard_map/reduce_sum | solution.py:10
  174.3 1.2 copy-done.2
  175.5 5.1 %multiply_add_fusion = f32[4096,512]{0,1:T(8,128)} fusion(f32[4096,512]{0,1:T(8,128)S(1)} %copy-done.2, f32[512]{0:T(512)S(1)} %bitcast.74, f32[512]{0:T(512)S(1)} %copy-done.21, f32[4096]{0:T(1024)S(1)} %add_rsqrt_fusion, f32[4096]{0:T(1024)S(1)} %broadcast_multiply_fusion), kind=kLoop, calls=%fused_computation.8 | loop fusion | flops 8388608 | bytes 16814080 | tf_op jit(solution)/shard_map/add | solution.py:11
  180.6 9.0 %copy.43 = f32[4096,512]{1,0:T(8,128)} copy(f32[4096,512]{0,1:T(8,128)} %multiply_add_fusion) | data formatting | bytes 16777216 | tf_op jit(solution)/shard_map/add | solution.py:11
  189.6 25.5 %scatter_custom_fusion.3 = f32[513,512]{1,0:T(8,128)S(1)} fusion(s32[4096]{0:T(1024)S(1)} %bitcast.71, f32[4096,512]{1,0:T(8,128)} %copy.43, f32[]{:T(128)} %constant.20.clone.1), kind=kCustom, calls=%fused_computation.49 | custom fusion | flops 2097152 | bytes 1051136 | tf_op jit(solution)/shard_map/scatter-add | solution.py:127
  215.1 0.9 slice.81
  216.1 7.2 %all_gather.27 = bf16[512,512]{1,0:T(8,128)(2,1)S(1)} all-gather(bf16[512,128]{1,0:T(8,128)(2,1)S(1)} %copy-done.10), channel_id=1, replica_groups=mesh['lat'=8,'lon'=4] {'lon'}, dimensions={1}, use_global_device_ids=true | all-gather | bytes 655360 | tf_op jit(solution)/shard_map/all_gather | solution.py:129
  223.3 30.2 %all-reduce.3.cloned.1.call-done = bf16[512,512]{1,0:T(8,128)(2,1)} async-done(((bf16[512,512]{1,0:T(8,128)(2,1)}), bf16[512,512]{1,0:T(8,128)(2,1)}) %all-reduce.3.cloned.1.call-update) | async-done | bytes 524304 | tf_op jit(solution)/shard_map/psum | solution.py:128
  253.5 2.4 convolution_convert_fusion.1
  255.9 0.3 all-gather.6.cloned.1.call-start
  256.2 0.5 all-gather.6.cloned.1.call-update
  256.7 0.1 reshape.137
  256.8 1.3 copy.44
  258.1 20.6 %all-gather.8.cloned.1.call-done = bf16[2048,512]{1,0:T(8,128)(2,1)} async-done(((bf16[512,512]{1,0:T(8,128)(2,1)}), bf16[2048,512]{1,0:T(8,128)(2,1)}) %all-gather.8.cloned.1.call-update) | async-done | bytes 2097168 | tf_op jit(solution)/shard_map/all_gather | solution.py:33
  278.8 2.2 reduce_sum.111
  281.0 0.2 convert_reduce_fusion.1
  281.1 0.3 fusion.9
  281.4 0.3 fusion.13
  281.8 2.6 gather_fusion
  284.4 5.5 %all-to-all-start.3 = ((bf16[8,64,512]{2,1,0:T(8,128)(2,1)}), bf16[8,64,512]{2,1,0:T(8,128)(2,1)S(1)}, u32[]{:S(2)}, u32[]{:S(2)}) async-start(bf16[8,64,512]{2,1,0:T(8,128)(2,1)} %bitcast.18), calls=%async_computation.3 | async-start | bytes 1048576 | tf_op jit(solution)/shard_map/all_to_all | solution.py:134
  290.0 10.9 %all_gather.33 = bf16[512,512]{1,0:T(8,128)(2,1)} all-gather(bf16[512,128]{1,0:T(8,128)(2,1)S(1)} %copy-done.11), channel_id=1, replica_groups=mesh['lat'=8,'lon'=4] {'lon'}, dimensions={1}, use_global_device_ids=true | all-gather | bytes 655360 | tf_op jit(solution)/shard_map/all_gather | solution.py:139
  300.9 2.0 all-gather.6.cloned.1.call-done
  303.0 3.1 fusion.29
  306.1 5.1 %gather_fusion.2 = bf16[1024,512]{1,0:T(8,128)(2,1)} fusion(bf16[512,512]{1,0:T(8,128)(2,1)S(1)} %fusion.13, s32[1024]{0:T(1024)S(1)} %fusion.57), kind=kCustom, calls=%fused_computation.3 | custom fusion | bytes 2101248 | tf_op jit(solution)/shard_map/gather | solution.py:137
  311.2 4.0 %gather_fusion.1 = bf16[1024,512]{1,0:T(8,128)(2,1)S(1)} fusion(bf16[1024,512]{1,0:T(8,128)(2,1)S(1)} %pad_maximum_fusion, s32[1024]{0:T(1024)S(1)} %fusion.56), kind=kCustom, calls=%fused_computation.2 | custom fusion | bytes 2101248 | tf_op jit(solution)/shard_map/gather | solution.py:136
  315.2 3.1 fusion.27
  318.3 4.3 %fusion.73 = (f32[1024]{0:T(1024)S(1)}, f32[1024,512]{0,1:T(8,128)S(1)}) fusion(bf16[512,512]{1,0:T(8,128)(2,1)S(1)} %copy-done.7, f32[1024,512]{1,0:T(8,128)} %fusion.29, f32[1024,512]{1,0:T(8,128)} %fusion.27, bf16[1024,512]{1,0:T(8,128)(2,1)} %gather_fusion.2, f32[512]{0:T(512)S(1)} %bitcast.79, bf16[1536,512]{1,0:T(8,128)(2,1)} %all-gather.6.cloned.1.call-done), kind=kOutput, calls=%fused_computation.113 | convolution fusion | flops 1078459392 | bytes 8394752 | tf_op jit(solution)/shard_map/dot_general | solution.py:149
  322.6 0.3 multiply_reduce_fusion.1
  322.9 0.9 copy-done.4
  323.8 0.5 add_convert_fusion
  324.4 1.0 copy-done.5
  325.3 1.5 fusion.6
  327.0 33.5 %all-reduce.5.cloned.1.call-done = bf16[512,512]{1,0:T(8,128)(2,1)} async-done(((bf16[512,512]{1,0:T(8,128)(2,1)}), bf16[512,512]{1,0:T(8,128)(2,1)}) %all-reduce.5.cloned.1.call-update) | async-done | bytes 524304 | tf_op jit(solution)/shard_map/psum | solution.py:158
  360.5 2.4 convolution_convert_fusion
  362.9 0.1 dynamic-slice.3
  363.0 0.8 dynamic-slice.2
  363.8 1.3 copy.45
  365.1 20.7 %all-gather.10.cloned.1.call-done = bf16[2048,512]{1,0:T(8,128)(2,1)} async-done(((bf16[512,512]{1,0:T(8,128)(2,1)}), bf16[2048,512]{1,0:T(8,128)(2,1)}) %all-gather.10.cloned.1.call-update) | async-done | bytes 2097168 | tf_op jit(solution)/shard_map/all_gather | solution.py:33
  385.7 2.2 reduce_sum.116
  388.0 0.1 convert_reduce_fusion
  388.1 0.3 multiply_reduce_fusion.2
  388.5 0.8 fusion.36
  (83 shorter events, 0.5 us)
Async XLA Ops:
  7.2 21.9 %copy-start = (bf16[512,512]{1,0:T(8,128)(2,1)S(1)}, bf16[512,512]{1,0:T(8,128)(2,1)}, u32[]{:S(2)}) copy-start(bf16[512,512]{1,0:T(8,128)(2,1)} %param.27) | copy-start | bytes 1572868
  21.0 29.3 %all-to-all-start = ((s32[8,1,512]{2,1,0:T(1,128)}), s32[8,1,512]{2,1,0:T(1,128)S(1)}, u32[]{:S(2)}, u32[]{:S(2)}) async-start(s32[8,1,512]{2,1,0:T(1,128)} %bitcast.5), calls=%async_computation | async-start | bytes 32768 | tf_op jit(solution)/shard_map/all_to_all | solution.py:116
  50.3 6.2 %copy-start.12 = (bf16[4,2048]{1,0:T(4,128)(2,1)S(1)}, bf16[4,2048]{1,0:T(4,128)(2,1)}, u32[]{:S(2)}) copy-start(bf16[4,2048]{1,0:T(4,128)(2,1)} %param.28) | copy-start | bytes 49156
  50.3 98.9 %all-to-all-start.1 = ((bf16[8,512,512]{2,1,0:T(8,128)(2,1)}), bf16[8,512,512]{2,1,0:T(8,128)(2,1)}, u32[]{:S(2)}, u32[]{:S(2)}) async-start(bf16[8,512,512]{2,1,0:T(8,128)(2,1)} %bitcast.59), calls=%async_computation.1 | async-start | bytes 8388608 | tf_op jit(solution)/shard_map/all_to_all | solution.py:102
  56.4 7.5 %copy-start.8 = (bf16[512,128]{1,0:T(8,128)(2,1)S(1)}, bf16[512,128]{1,0:T(8,128)(2,1)}, u32[]{:S(2)}) copy-start(bf16[512,128]{1,0:T(8,128)(2,1)} %param.37) | copy-start | bytes 393220
  56.4 14.7 %copy-start.9 = (bf16[512,128]{1,0:T(8,128)(2,1)S(1)}, bf16[512,128]{1,0:T(8,128)(2,1)}, u32[]{:S(2)}) copy-start(bf16[512,128]{1,0:T(8,128)(2,1)} %param.39) | copy-start | bytes 393220
  56.5 21.9 %copy-start.13 = (f32[2,512]{1,0:T(2,128)S(1)}, f32[2,512]{1,0:T(2,128)}, u32[]{:S(2)}) copy-start(f32[2,512]{1,0:T(2,128)} %param.40) | copy-start | bytes 12292
  56.5 21.9 %copy-start.14 = (f32[2,512]{1,0:T(2,128)S(1)}, f32[2,512]{1,0:T(2,128)}, u32[]{:S(2)}) copy-start(f32[2,512]{1,0:T(2,128)} %param.44) | copy-start | bytes 12292
  149.2 11.6 %all-to-all-start.2 = ((bf16[8,512,4]{1,2,0:T(4,128)(2,1)}), bf16[8,512,4]{1,2,0:T(4,128)(2,1)S(1)}, u32[]{:S(2)}, u32[]{:S(2)}) async-start(bf16[8,512,4]{1,2,0:T(4,128)(2,1)} %copy.42), calls=%async_computation.2 | async-start | bytes 65536 | tf_op jit(solution)/shard_map/all_to_all | solution.py:109
  152.8 100.7 %all-reduce.3.cloned.1.call-start = ((), (), s32[]{:S(2)}) async-start(), calls=%async_computation.4 | async-start | bytes 1048576 | tf_op jit(solution)/shard_map/psum | solution.py:128
  153.0 7.8 %copy-start.27 = (bf16[4,512]{1,0:T(4,128)(2,1)S(1)}, bf16[4,512]{1,0:T(4,128)(2,1)}, u32[]{:S(2)}) copy-start(bf16[4,512]{1,0:T(4,128)(2,1)} %param.38) | copy-start | bytes 12292
  169.7 5.8 %copy-start.2 = (f32[4096,512]{0,1:T(8,128)S(1)}, f32[4096,512]{0,1:T(8,128)}, u32[]{:S(2)}) copy-start(f32[4096,512]{0,1:T(8,128)} %get-tuple-element.21) | copy-start | bytes 25165828
  169.7 5.8 %copy-start.21 = (f32[512]{0:T(512)S(1)}, f32[512]{0:T(512)}, u32[]{:S(2)}) copy-start(f32[512]{0:T(512)} %param.41) | copy-start | bytes 6148
  189.6 26.5 %copy-start.10 = (bf16[512,128]{1,0:T(8,128)(2,1)S(1)}, bf16[512,128]{1,0:T(8,128)(2,1)}, u32[]{:S(2)}) copy-start(bf16[512,128]{1,0:T(8,128)(2,1)} %param.32) | copy-start | bytes 393220
  189.6 63.9 %copy-start.23 = (bf16[1024,128]{1,0:T(8,128)(2,1)S(1)}, bf16[1024,128]{1,0:T(8,128)(2,1)}, u32[]{:S(2)}) copy-start(bf16[1024,128]{1,0:T(8,128)(2,1)} %param.42) | copy-start | bytes 786436
  189.6 63.9 %copy-start.25 = (bf16[128,512]{1,0:T(8,128)(2,1)S(1)}, bf16[128,512]{1,0:T(8,128)(2,1)}, u32[]{:S(2)}) copy-start(bf16[128,512]{1,0:T(8,128)(2,1)} %param.43) | copy-start | bytes 393220
  216.0 62.7 %all-gather.8.cloned.1.call-start = ((), (), s32[]{:S(2)}) async-start(), calls=%async_computation.7 | async-start | bytes 2621440 | tf_op jit(solution)/shard_map/all_gather | solution.py:33
  223.3 33.4 %copy-start.15 = (s32[8,64]{1,0:T(8,128)S(1)}, s32[8,64]{1,0:T(8,128)}, u32[]{:S(2)}) copy-start(s32[8,64]{1,0:T(8,128)} %param.34) | copy-start | bytes 6148
  223.3 33.5 %copy-start.3 = (bf16[1024,512]{1,0:T(8,128)(2,1)S(1)}, bf16[1024,512]{1,0:T(8,128)(2,1)}, u32[]{:S(2)}) copy-start(bf16[1024,512]{1,0:T(8,128)(2,1)} %param.33) | copy-start | bytes 3145732
  255.9 2.2 copy-start.16
  255.9 47.0 %all-gather.6.cloned.1.call-start = ((), (), s32[]{:S(2)}) async-start(), calls=%async_computation.5 | async-start | bytes 1966080 | tf_op jit(solution)/shard_map/all_gather | solution.py:138
  258.1 23.3 %copy-start.22 = (f32[512]{0:T(512)S(1)}, f32[512]{0:T(512)}, u32[]{:S(2)}) copy-start(f32[512]{0:T(512)} %param.45) | copy-start | bytes 6148
  281.8 8.2 %copy-start.11 = (bf16[512,128]{1,0:T(8,128)(2,1)S(1)}, bf16[512,128]{1,0:T(8,128)(2,1)}, u32[]{:S(2)}) copy-start(bf16[512,128]{1,0:T(8,128)(2,1)} %param.47) | copy-start | bytes 393220
  281.8 19.1 %copy-start.18 = (s32[1024]{0:T(1024)S(1)}, s32[1024]{0:T(1024)}, u32[]{:S(2)}) copy-start(s32[1024]{0:T(1024)} %param.36) | copy-start | bytes 12292
  281.8 19.1 %copy-start.17 = (f32[2,512]{1,0:T(2,128)S(1)}, f32[2,512]{1,0:T(2,128)}, u32[]{:S(2)}) copy-start(f32[2,512]{1,0:T(2,128)} %param.48) | copy-start | bytes 12292
  284.4 26.7 %all-to-all-start.3 = ((bf16[8,64,512]{2,1,0:T(8,128)(2,1)}), bf16[8,64,512]{2,1,0:T(8,128)(2,1)S(1)}, u32[]{:S(2)}, u32[]{:S(2)}) async-start(bf16[8,64,512]{2,1,0:T(8,128)(2,1)} %bitcast.18), calls=%async_computation.3 | async-start | bytes 1048576 | tf_op jit(solution)/shard_map/all_to_all | solution.py:134
  290.0 70.5 %all-reduce.5.cloned.1.call-start = ((), (), s32[]{:S(2)}) async-start(), calls=%async_computation.6 | async-start | bytes 1048576 | tf_op jit(solution)/shard_map/psum | solution.py:158
  315.2 3.1 copy-start.7
  322.6 1.2 copy-start.4
  322.6 1.2 copy-start.20
  324.4 1.0 copy-start.5
  325.3 1.6 copy-start.19
  325.3 35.2 %copy-start.24 = (bf16[1024,128]{1,0:T(8,128)(2,1)S(1)}, bf16[1024,128]{1,0:T(8,128)(2,1)}, u32[]{:S(2)}) copy-start(bf16[1024,128]{1,0:T(8,128)(2,1)} %param.50) | copy-start | bytes 786436
  325.3 35.2 %copy-start.26 = (bf16[128,512]{1,0:T(8,128)(2,1)S(1)}, bf16[128,512]{1,0:T(8,128)(2,1)}, u32[]{:S(2)}) copy-start(bf16[128,512]{1,0:T(8,128)(2,1)} %param.51) | copy-start | bytes 393220
  326.9 58.9 %all-gather.10.cloned.1.call-start = ((), (), s32[]{:S(2)}) async-start(), calls=%async_computation.8 | async-start | bytes 2621440 | tf_op jit(solution)/shard_map/all_gather | solution.py:33
  327.0 36.8 %copy-start.6 = (bf16[1024,512]{0,1:T(8,128)(2,1)S(1)}, bf16[1024,512]{0,1:T(8,128)(2,1)}, u32[]{:S(2)}) copy-start(bf16[1024,512]{0,1:T(8,128)(2,1)} %copy-done.5) | copy-start | bytes 3145732
  385.7 3.5 copy-start.1
Sparse Core Ops, SparseCore 0:
  216.1 37.3 all-reduce.2
  256.1 22.6 all-gather.7
  280.3 22.6 all-gather.5
  327.0 33.4 all-reduce.4
  363.0 22.6 all-gather.9
